TPU v7x, 32 devices: a whole 2x2x4 slice. The times are simulated.
32 devices in a mesh: ep: 16 (over z, y, x), tp: 2 (over core).
Axes of the slice: x: 2, y: 2, z: 4, core: 2. Of those that a mesh axis runs over, the one named last changes fastest.
Arguments:
- tokens: bfloat16 [2048, 3584], P('ep'), may hold values from -6 to 6
- expert_ids: int32 [2048, 8], P('ep'), may hold values from 0 to 15, all different within a row; in each aligned block of 128 rows (0 to 127, 128 to 255, ...) at most 96 rows name the same one
- gate_values: float32 [2048, 8], P('ep'), may hold values from 0.05 to 1
- w_gate: bfloat16 [16, 3584, 1024], P('ep', None, 'tp'), may hold values from -0.09375 to 0.09375
- w_up: bfloat16 [16, 3584, 1024], P('ep', None, 'tp'), may hold values from -0.09375 to 0.09375
- w_down: bfloat16 [16, 1024, 3584], P('ep', 'tp'), may hold values from -0.1875 to 0.1875
- shared_gate: bfloat16 [3584, 1024], P(None, 'tp'), may hold values from -0.09375 to 0.09375
- shared_up: bfloat16 [3584, 1024], P(None, 'tp'), may hold values from -0.09375 to 0.09375
- shared_down: bfloat16 [1024, 3584], P('tp'), may hold values from -0.1875 to 0.1875
Outputs:
- layer_out: bfloat16 [2048, 3584], P('ep', 'tp')
Inputs may be any that keep to these rules, and one draw needn't show every extreme that they name: `expert_ids`: each row names 8 different experts; within the rows of one index of ep (aligned blocks of 128 rows) no expert is named by more than 96 rows.
All inputs are finite; a program needn't handle non-finite values.
Results may differ from a plain program's by a relative error of at most 0.0085.
Values may be sent and summed in bfloat16 or wider, within the bound.
A program may use at most 128 MiB of HBM per device.

v0:
```python
import jax
import jax.numpy as jnp
from jax import lax
from jax.sharding import PartitionSpec as P

route_scale = 2.827


def expert_apply(inputs, gate_matrix, up_matrix, down_matrix):
    gate_out = jnp.dot(inputs, gate_matrix, preferred_element_type=jnp.float32)
    up_out = jnp.dot(inputs, up_matrix, preferred_element_type=jnp.float32)
    hidden = (jax.nn.silu(gate_out) * up_out).astype(jnp.bfloat16)
    return jnp.dot(hidden, down_matrix, preferred_element_type=jnp.float32)


def combine_rows(returned, target, weights, tok_rows, top_count):
    feature_count = returned.shape[-1]
    picked = jnp.take(returned.reshape(-1, feature_count), target, axis=0)
    picked = picked.reshape(tok_rows, top_count, feature_count)
    return jnp.sum(picked * weights[:, :, None], axis=1)


def per_device(
    tokens, expert_ids, gate_values, w_gate, w_up, w_down, shared_gate, shared_up, shared_down
):
    ep_count = lax.axis_size("ep")
    tp_count = lax.axis_size("tp")
    tok_rows, model_width = tokens.shape
    top_count = expert_ids.shape[1]
    experts = ep_count * w_gate.shape[0]
    capacity = 3 * tok_rows * top_count // (2 * experts)
    weights = route_scale * gate_values / jnp.sum(gate_values, axis=1, keepdims=True)
    flat_ids = expert_ids.reshape(-1)
    onehot = (flat_ids[:, None] == jnp.arange(experts, dtype=jnp.int32)[None, :]).astype(jnp.int32)
    earlier = jnp.cumsum(onehot, axis=0) - onehot
    slot_index = jnp.sum(earlier * onehot, axis=1)
    target = flat_ids * capacity + slot_index
    row_owner = jnp.full((experts * capacity,), tok_rows, jnp.int32)
    row_owner = row_owner.at[target].set(
        jnp.arange(flat_ids.shape[0], dtype=jnp.int32) // top_count
    )
    half_width = model_width // tp_count
    source = lax.dynamic_slice_in_dim(tokens, lax.axis_index("tp") * half_width, half_width, 1)
    padded = jnp.concatenate([source, jnp.zeros((1, source.shape[1]), jnp.bfloat16)], axis=0)
    outgoing = jnp.take(padded, row_owner, axis=0).reshape(ep_count, capacity, source.shape[1])
    parted = lax.all_to_all(outgoing, "ep", split_axis=0, concat_axis=0, tiled=True)
    arrived = lax.all_gather(parted, "tp", axis=2, tiled=True)
    expert_rows = arrived.reshape(-1, model_width)
    partial_value = expert_apply(expert_rows, w_gate[0], w_up[0], w_down[0])
    shared = expert_apply(tokens, shared_gate, shared_up, shared_down)
    returned = lax.all_to_all(
        partial_value.reshape(ep_count, capacity, model_width).astype(jnp.bfloat16),
        "ep",
        split_axis=0,
        concat_axis=0,
        tiled=True,
    ).astype(jnp.float32)
    routed = combine_rows(returned, target, weights, tok_rows, top_count)
    return lax.psum_scatter(routed + shared, "tp", scatter_dimension=1, tiled=True).astype(
        jnp.bfloat16
    )


def solution(mesh):
    return jax.shard_map(
        per_device,
        mesh=mesh,
        in_specs=(
            P("ep", None),
            P("ep", None),
            P("ep", None),
            P("ep", None, "tp"),
            P("ep", None, "tp"),
            P("ep", "tp", None),
            P(None, "tp"),
            P(None, "tp"),
            P("tp", None),
        ),
        out_specs=P("ep", "tp"),
        check_vma=False,
    )
```

profile of v0, /device:TPU:0, one launch (start us, length us, event | category | flops | bytes accessed | tf_op | source)
XLA Modules:
  0.0 533.9 jit_solution(1072391069234438382)
XLA Ops:
  6.5 0.9 copy.20
  7.4 0.1 eq.26
  7.5 0.1 reshape.87
  7.6 0.7 broadcast_multiply_fusion
  8.3 4.5 reduce-window.6
  12.8 0.1 slice.12
  12.9 0.1 copy.22
  13.1 0.1 broadcast_add_fusion
  13.2 0.1 copy.26
  13.3 0.1 mul.56
  13.5 4.3 scatter_custom_fusion
  17.9 0.1 broadcast_in_dim.34
  18.0 6.7 %gather_fusion = bf16[1536,1792]{1,0:T(8,128)(2,1)} fusion(bf16[129,1792]{1,0:T(8,128)(2,1)S(1)} %concatenate.3, s32[2048]{0:T(1024)S(1)} %pad_clamp_fusion), kind=kCustom, calls=%fused_computation | custom fusion | bytes 11016192 | tf_op jit(solution)/shard_map/jit(_take)/gather | solution.py:45
  24.7 3.1 broadcast_select_fusion
  27.9 130.6 %all_to_all.10 = bf16[16,96,1792]{2,1,0:T(8,128)(2,1)} all-to-all(bf16[16,96,1792]{2,1,0:T(8,128)(2,1)S(1)} %broadcast_select_fusion), channel_id=1, replica_groups=mesh['ep'=16,'tp'=2] {'ep'}, dimensions={0} | all-to-all | bytes 11010048 | tf_op jit(solution)/shard_map/all_to_all | solution.py:46
  158.5 21.1 %all-gather.2.cloned.1.call-done = bf16[16,96,3584]{2,1,0:T(8,128)(2,1)} async-done(((bf16[16,96,1792]{2,1,0:T(8,128)(2,1)}), bf16[16,96,3584]{2,1,0:T(8,128)(2,1)}) %all-gather.2.cloned.1.call-update) | async-done | bytes 11010064 | tf_op jit(solution)/shard_map/all_gather | solution.py:47
  179.6 9.8 %fusion.5 = f32[1536,512]{1,0:T(8,128)S(1)} fusion(bf16[1536,3584]{1,0:T(8,128)(2,1)} %bitcast.60, bf16[1,3584,512]{2,1,0:T(8,128)(2,1)} %param.12), kind=kOutput, calls=%fused_computation.13 | convolution fusion | flops 5637144576 | bytes 17825792 | tf_op jit(solution)/shard_map/dot_general | solution.py:10
  189.5 6.5 %fusion.10 = bf16[1536,512]{1,0:T(8,128)(2,1)S(1)} fusion(bf16[1536,3584]{1,0:T(8,128)(2,1)S(1)} %bitcast.61, bf16[1,3584,512]{2,1,0:T(8,128)(2,1)S(1)} %copy-done.4, f32[1536,512]{1,0:T(8,128)S(1)} %fusion.5), kind=kOutput, calls=%fused_computation.16 | convolution fusion | flops 5641863168 | bytes 19398656 | tf_op jit(solution)/shard_map/dot_general | solution.py:11
  196.0 8.5 %convolution_convert_fusion = bf16[16,96,3584]{2,1,0:T(8,128)(2,1)} fusion(bf16[16,96,512]{2,1,0:T(8,128)(2,1)S(1)} %bitcast.62, bf16[1,512,3584]{2,1,0:T(8,128)(2,1)S(1)} %copy-done.5), kind=kOutput, calls=%fused_computation.7 | convolution fusion | flops 5642649600 | bytes 16252928 | tf_op jit(solution)/shard_map/dot_general | solution.py:13
  204.5 7.0 %all-to-all-start.1 = ((bf16[16,96,3584]{2,1,0:T(8,128)(2,1)}), bf16[16,96,3584]{2,1,0:T(8,128)(2,1)}, u32[]{:S(2)}, u32[]{:S(2)}) async-start(bf16[16,96,3584]{2,1,0:T(8,128)(2,1)} %convolution_convert_fusion), calls=%async_computation.1 | async-start | bytes 22020096 | tf_op jit(solution)/shard_map/all_to_all | solution.py:51
  211.5 0.3 reduce-scatter.2.cloned.1.call-start
  211.7 0.1 reduce_sum.32
  211.9 0.1 copy.25
  212.1 0.1 copy.27
  212.2 2.7 fusion.30
  214.9 205.1 %all-to-all-done.1 = bf16[16,96,3584]{2,1,0:T(8,128)(2,1)} async-done(((bf16[16,96,3584]{2,1,0:T(8,128)(2,1)}), bf16[16,96,3584]{2,1,0:T(8,128)(2,1)}, u32[]{:S(2)}, u32[]{:S(2)}) %all-to-all-start.1) | async-done | bytes 11010080 | tf_op jit(solution)/shard_map/all_to_all | solution.py:51
  420.0 12.5 %bitcast_convert_fusion = f32[1536,3584]{1,0:T(8,128)} fusion(bf16[16,96,3584]{2,1,0:T(8,128)(2,1)} %all-to-all-done.1), kind=kLoop, calls=%fused_computation.6 | loop fusion | flops 5505024 | bytes 33030144 | tf_op jit(solution)/shard_map/reshape | solution.py:18
  432.5 20.7 %gather_fusion.1 = f32[1024,3584]{1,0:T(8,128)} fusion(f32[1536,3584]{1,0:T(8,128)} %bitcast_convert_fusion, s32[1024]{0:T(1024)S(1)} %broadcast_clamp_fusion), kind=kCustom, calls=%fused_computation.1 | custom fusion | bytes 29364224 | tf_op jit(solution)/shard_map/jit(_take)/gather | solution.py:18
  453.2 13.9 %fusion.1 = f32[128,3584]{1,0:T(8,128)S(1)} fusion(f32[1024,3584]{1,0:T(8,128)} %gather_fusion.1, f32[128,8]{1,0:T(8,128)S(1)} %copy.27, pred[128,8]{1,0:T(8,128)(4,1)S(1)} %copy.25), kind=kLoop, calls=%fused_computation.5 | loop fusion | flops 10551296 | bytes 16520192 | tf_op jit(solution)/shard_map/reduce_sum | solution.py:20
  467.1 5.7 %convolution_add_fusion = f32[128,3584]{1,0:T(8,128)} fusion(f32[128,3584]{1,0:T(8,128)S(1)} %fusion.1, bf16[512,3584]{1,0:T(8,128)(2,1)} %param.17, bf16[128,3584]{1,0:T(8,128)(2,1)S(1)} %copy-done, bf16[3584,512]{1,0:T(8,128)(2,1)} %param.16, f32[128,512]{1,0:T(8,128)S(1)} %fusion.30), kind=kOutput, calls=%fused_computation.9 | convolution fusion | flops 940376064 | bytes 12189696 | tf_op jit(solution)/shard_map/dot_general | solution.py:13
  472.8 52.3 %reduce-scatter.2.cloned.1.call-done = f32[128,1792]{1,0:T(8,128)} async-done(((f32[128,3584]{1,0:T(8,128)}), f32[128,1792]{1,0:T(8,128)}) %reduce-scatter.2.cloned.1.call-update) | async-done | bytes 917520 | tf_op jit(solution)/shard_map/reduce_scatter | solution.py:59
  525.1 2.0 convert_element_type.25
  (32 shorter events, 0.4 us)
Async XLA Ops:
  6.5 11.4 %copy-start = (bf16[128,3584]{1,0:T(8,128)(2,1)S(1)}, bf16[128,3584]{1,0:T(8,128)(2,1)}, u32[]{:S(2)}) copy-start(bf16[128,3584]{1,0:T(8,128)(2,1)} %param.9) | copy-start | bytes 2752516
  6.5 173.1 %all-gather.2.cloned.1.call-start = ((), (), s32[]{:S(2)}) async-start(), calls=%async_computation.3 | async-start | bytes 16515072 | tf_op jit(solution)/shard_map/all_gather | solution.py:47
  179.6 9.8 %copy-start.3 = (bf16[16,96,3584]{2,1,0:T(8,128)(2,1)S(1)}, bf16[16,96,3584]{2,1,0:T(8,128)(2,1)}, u32[]{:S(2)}) copy-start(bf16[16,96,3584]{2,1,0:T(8,128)(2,1)} %all-gather.2.cloned.1.call-done) | copy-start | bytes 33030148
  179.6 9.8 %copy-start.4 = (bf16[1,3584,512]{2,1,0:T(8,128)(2,1)S(1)}, bf16[1,3584,512]{2,1,0:T(8,128)(2,1)}, u32[]{:S(2)}) copy-start(bf16[1,3584,512]{2,1,0:T(8,128)(2,1)} %param.13) | copy-start | bytes 11010052
  189.4 6.5 %copy-start.5 = (bf16[1,512,3584]{2,1,0:T(8,128)(2,1)S(1)}, bf16[1,512,3584]{2,1,0:T(8,128)(2,1)}, u32[]{:S(2)}) copy-start(bf16[1,512,3584]{2,1,0:T(8,128)(2,1)} %param.14) | copy-start | bytes 11010052
  204.5 7.4 %copy-start.1 = (s32[128,8]{0,1:T(8,128)S(1)}, s32[128,8]{0,1:T(8,128)}, u32[]{:S(2)}) copy-start(s32[128,8]{0,1:T(8,128)} %param.10) | copy-start | bytes 12292
  204.5 7.5 %copy-start.2 = (f32[128,8]{0,1:T(8,128)S(1)}, f32[128,8]{0,1:T(8,128)}, u32[]{:S(2)}) copy-start(f32[128,8]{0,1:T(8,128)} %param.11) | copy-start | bytes 12292
  204.5 215.5 %all-to-all-start.1 = ((bf16[16,96,3584]{2,1,0:T(8,128)(2,1)}), bf16[16,96,3584]{2,1,0:T(8,128)(2,1)}, u32[]{:S(2)}, u32[]{:S(2)}) async-start(bf16[16,96,3584]{2,1,0:T(8,128)(2,1)} %convolution_convert_fusion), calls=%async_computation.1 | async-start | bytes 22020096 | tf_op jit(solution)/shard_map/all_to_all | solution.py:51
  211.5 313.6 %reduce-scatter.2.cloned.1.call-start = ((), (), s32[]{:S(2)}) async-start(), calls=%async_computation.4 | async-start | bytes 2752512 | tf_op jit(solution)/shard_map/reduce_scatter | solution.py:59
Sparse Core Ops, SparseCore 0:
  158.7 20.8 all-gather.1
  472.9 52.1 reduce-scatter.1
where the time goes:
time: 534 us
  waiting for transfers between devices  278 us (52%)
  blocking collectives  131 us (25%)
  other arithmetic  36.9 us (7%)
  local copies, waits for them, and re-layouts  33.8 us (6%)
  matrix products  33.2 us (6%)
  between operations  13.6 us (3%)
  starting transfers between devices  7.23 us (1%)
    all_to_all x1, waiting for transfers between devices, per_device(): lax.all_to_all(partial_value.reshape(ep_count, capacity, model_width).ast...  205 us
    all_to_all x1, blocking collectives, per_device(): lax.all_to_all(outgoing, 'ep', split_axis=0, concat_axis=0, tiled=True)  131 us
    reduce_scatter x1, waiting for transfers between devices, per_device(): lax.psum_scatter(routed + shared, 'tp', scatter_dimension=1, tiled=True)  52.3 us
    all_gather x1, waiting for transfers between devices, per_device(): arrived = lax.all_gather(parted, 'tp', axis=2, tiled=True)  21.1 us
    gather x1, local copies, waits for them, and re-layouts, combine_rows(): picked = jnp.take(returned.reshape(-1, feature_count), target, axis=0)  20.7 us
    dot_general x2, matrix products, expert_apply(): return jnp.dot(hidden, down_matrix, preferred_element_type=jnp.float32)  14.2 us
    reduce_sum x1, other arithmetic, combine_rows(): return jnp.sum(picked * weights[:, :, None], axis=1)  13.9 us
    dot_general x2, matrix products, expert_apply(): gate_out = jnp.dot(inputs, gate_matrix, preferred_element_type=jnp.float32)  12.5 us
  transfers between devices with their start and end apart: 3, of which 3 were waited for; matrix products, arithmetic and copies ran while one was open for 1% of the time, Pallas kernels for 0%

commit v1 on v0

--- a/solution.py
+++ b/solution.py
@@ -1,6 +1,11 @@
+import functools
+import math
+
 import jax
 import jax.numpy as jnp
 from jax import lax
+from jax.experimental import pallas as pl
+from jax.experimental.pallas import tpu as pltpu
 from jax.sharding import PartitionSpec as P
 
 route_scale = 2.827
@@ -20,7 +25,7 @@
     return jnp.sum(picked * weights[:, :, None], axis=1)
 
 
-def per_device(
+def per_device_routed(
     tokens, expert_ids, gate_values, w_gate, w_up, w_down, shared_gate, shared_up, shared_down
 ):
     ep_count = lax.axis_size("ep")
@@ -61,6 +66,400 @@
     )
 
 
+MESH = pl.DeviceIdType.MESH
+LANES = 128
+VMEM_BYTES = 66_000_000
+
+
+def ring_order(position):
+    return position + (position // 2 % 2) * (1 - 2 * (position % 2))
+
+
+def fused_kernel(
+    side, tok, tab, w_gate, w_up, w_down, s_gate, s_up, s_down, out,
+    x, table, own, away, peer, hidden, gate_w, up_w, down_w,
+    shared_own, shared_away, shared_peer, ring1, ring2,
+    local_sem, arrive, cross, plane_recv, ring1_recv, ring2_recv, send_sem,
+):
+    rows = tok.shape[0]
+    half_rows = rows // 2
+    half = tok.shape[1] // 2
+    part = half // 2
+    fe = w_gate.shape[1]
+    me = lax.axis_index("ep")
+    core = lax.axis_index("tp")
+    zpos = me // side
+    ppos = ring_order(me % side)
+
+    def block_of(p, z):
+        return lax.rem(z + 2 * side, side) * side + ring_order(lax.rem(p + 2 * side, side))
+
+    def neighbour(axis, step):
+        if axis == 0:
+            return {"ep": block_of(ppos + step, zpos)}
+        return {"ep": block_of(ppos, zpos + step)}
+
+    partner = {"tp": 1 - core}
+    barrier = pltpu.get_barrier_semaphore()
+    for axis in (0, 1):
+        for step in (1, -1):
+            pl.semaphore_signal(barrier, inc=1, device_id=neighbour(axis, step), device_id_type=MESH)
+    pl.semaphore_signal(barrier, inc=1, device_id=partner, device_id_type=MESH)
+
+    def load(sources):
+        copies = []
+        for number, (src, dst) in enumerate(zip(sources, (gate_w, up_w, down_w))):
+            copy = pltpu.make_async_copy(src, dst, local_sem.at[number])
+            copy.start()
+            copies.append(copy)
+        return copies
+
+    mine = pltpu.make_async_copy(tok, x.at[pl.ds(pl.multiple_of(me * rows, rows), rows)], local_sem.at[3])
+    mine_table = pltpu.make_async_copy(tab, table.at[me], local_sem.at[4])
+    mine.start()
+    mine_table.start()
+    shared_copies = load((s_gate, s_up, s_down))
+    mine.wait()
+    mine_table.wait()
+    pl.semaphore_wait(barrier, 5)
+
+    pending = []
+
+    def send(src, dst, recv_sem, device):
+        copy = pltpu.make_async_remote_copy(
+            src_ref=src, dst_ref=dst, send_sem=send_sem.at[len(pending)], recv_sem=recv_sem,
+            device_id=device, device_id_type=MESH,
+        )
+        copy.start()
+        pending.append(copy)
+
+    def arrived(ref, recv_sem):
+        pltpu.make_async_remote_copy(
+            src_ref=ref, dst_ref=ref, send_sem=send_sem.at[0], recv_sem=recv_sem,
+            device_id=partner, device_id_type=MESH,
+        ).wait_recv()
+
+    def piece(block, s, v, which):
+        if s == 2:
+            return table.at[block]
+        column = pl.multiple_of(which * half + s * part, LANES)
+        return x.at[pl.ds(pl.multiple_of(block * rows + v * half_rows, half_rows), half_rows), pl.ds(column, part)]
+
+    def hops(v):
+        ahead = side // 2 if v == 0 else (side - 1) // 2
+        return ahead, side - 1 - ahead
+
+    streams = [(0, 0), (1, 0), (0, 1), (1, 1), (2, 0)]
+
+    def axes(s):
+        return (1, 0) if s == 1 else (0, 1)
+
+    def at(s, first, second):
+        if axes(s)[0] == 0:
+            return block_of(ppos + first, zpos + second)
+        return block_of(ppos + second, zpos + first)
+
+    def forward(s, v, first, second, axis, step):
+        block = at(s, first, second)
+        ref = piece(block, s, v, core)
+        send(ref, ref, arrive.at[s, v, block], neighbour(axis, step))
+
+    def receive(s, v, first, second):
+        block = at(s, first, second)
+        ref = piece(block, s, v, core)
+        arrived(ref, arrive.at[s, v, block])
+        if s < 2:
+            send(ref, ref, cross.at[s, v, block], partner)
+
+    def reach(v, step):
+        ahead, back = hops(v)
+        return ahead if step == 1 else back
+
+    def fan(s, v, first):
+        for step in (1, -1):
+            if reach(v, step) >= 1:
+                forward(s, v, first, 0, axes(s)[1], step)
+
+    for s, v in streams:
+        for step in (1, -1):
+            if reach(v, step) >= 1:
+                forward(s, v, 0, 0, axes(s)[0], step)
+    for s, v in streams:
+        fan(s, v, 0)
+    longest = side // 2
+    for k in range(1, longest + 1):
+        for s, v in streams:
+            for step in (1, -1):
+                if k <= reach(v, step):
+                    receive(s, v, -step * k, 0)
+                    if k < reach(v, step):
+                        forward(s, v, -step * k, 0, axes(s)[0], step)
+                    fan(s, v, -step * k)
+
+    firsts = [0]
+    for k in range(1, longest + 1):
+        firsts += [-k, k]
+    firsts = firsts[:side]
+
+    def second_phase(k, group):
+        for first in group:
+            for s, v in streams:
+                for step in (1, -1):
+                    if k <= reach(v, step):
+                        position = first
+                        receive(s, v, position, -step * k)
+                        if k < reach(v, step):
+                            forward(s, v, position, -step * k, axes(s)[1], step)
+
+    def swiglu(inputs, columns):
+        gate = jnp.dot(inputs, gate_w[:, columns], preferred_element_type=jnp.float32)
+        up = jnp.dot(inputs, up_w[:, columns], preferred_element_type=jnp.float32)
+        return gate / (1.0 + jnp.exp(-gate)) * up
+
+    tile = 256
+    for copy in shared_copies:
+        copy.wait()
+
+    @pl.loop(0, fe // tile)
+    def _(j):
+        columns = pl.ds(pl.multiple_of(j * tile, tile), tile)
+        inputs = x[pl.ds(pl.multiple_of(me * rows, rows), rows), :]
+        hidden[0:rows, columns] = swiglu(inputs, columns).astype(jnp.bfloat16)
+
+    @pl.loop(0, half // tile)
+    def _(j):
+        columns = pl.ds(pl.multiple_of(j * tile, tile), tile)
+        mine_columns = pl.ds(pl.multiple_of(core * half + j * tile, tile), tile)
+        other_columns = pl.ds(pl.multiple_of((1 - core) * half + j * tile, tile), tile)
+        h = hidden[0:rows, :]
+        shared_own[:, columns] = jnp.dot(h, down_w[:, mine_columns], preferred_element_type=jnp.float32)
+        shared_away[:, columns] = jnp.dot(h, down_w[:, other_columns], preferred_element_type=jnp.float32)
+
+    send(shared_away, shared_peer, plane_recv.at[side], partner)
+    expert_copies = load((w_gate, w_up, w_down))
+
+    for k in range(1, longest + 1):
+        second_phase(k, firsts)
+    for block_step in range(1, side * side):
+        block = lax.rem(me + block_step, side * side)
+        for s in (0, 1):
+            for v in (0, 1):
+                arrived(piece(block, s, v, 1 - core), cross.at[s, v, block])
+    for copy in expert_copies:
+        copy.wait()
+
+    group = 2 * rows
+
+    def plane(offset):
+        z = lax.rem(zpos + offset + side, side)
+
+        @pl.loop(0, side // 2)
+        def _(m):
+            start = pl.multiple_of((z * side + 2 * m) * rows, group)
+            columns_of = []
+            for b in range(2):
+                values = table[z * side + 2 * m + b]
+                lines = lax.broadcasted_iota(jnp.int32, values.shape, 0)
+                line = jnp.sum(jnp.where(lines == me, values, 0.0), axis=0, keepdims=True)
+                columns_of.append(jnp.broadcast_to(line, (rows, rows)).T[:, :1])
+            weight = jnp.concatenate(columns_of, axis=0)
+
+            @pl.loop(0, fe // tile)
+            def _(j):
+                columns = pl.ds(pl.multiple_of(j * tile, tile), tile)
+                value = swiglu(x[pl.ds(start, group), :], columns) * weight
+                hidden[pl.ds(pl.multiple_of(m * group, group), group), columns] = value.astype(jnp.bfloat16)
+
+        @pl.loop(0, half // tile)
+        def _(j):
+            columns = pl.ds(pl.multiple_of(j * tile, tile), tile)
+            mine_columns = pl.ds(pl.multiple_of(core * half + j * tile, tile), tile)
+            other_columns = pl.ds(pl.multiple_of((1 - core) * half + j * tile, tile), tile)
+            h = hidden[...]
+            value = jnp.dot(h, down_w[:, other_columns], preferred_element_type=jnp.float32)
+            away[z, :, :, columns] = value.astype(jnp.bfloat16).reshape(side, rows, tile)
+            value = jnp.dot(h, down_w[:, mine_columns], preferred_element_type=jnp.float32)
+            own[z, :, :, columns] = value.astype(jnp.bfloat16).reshape(side, rows, tile)
+
+        send(away.at[z], peer.at[z], plane_recv.at[z], partner)
+
+    def join(offset):
+        z = lax.rem(zpos + offset + side, side)
+        arrived(peer.at[z], plane_recv.at[z])
+
+        @pl.loop(0, side)
+        def _(b):
+            total = own[z, b].astype(jnp.float32) + peer[z, b].astype(jnp.float32)
+            own[z, b] = total.astype(jnp.bfloat16)
+
+    planes = [firsts[-1]] + firsts[1:-1] + [0] if side > 1 else [0]
+
+    def own_piece(s, v, target, inner):
+        spot = pl.ds(v * half_rows, half_rows), pl.ds(s * part, part)
+        if s == 0:
+            return (lax.rem(zpos + target + 2 * side, side), inner) + spot
+        return (inner, ring_order(lax.rem(ppos + target + 2 * side, side))) + spot
+
+    def slot_of(v, step, k):
+        return k - 1 if step == 1 else reach(v, 1) + k - 1
+
+    def add_into(s, v, target, slots):
+        @pl.loop(0, side)
+        def _(inner):
+            index = own_piece(s, v, target, inner)
+            total = own[index].astype(jnp.float32)
+            for slot in slots:
+                total += ring1[s, v, slot, inner].astype(jnp.float32)
+            own[index] = total.astype(jnp.bfloat16)
+
+    def ring1_step(s, v, step, k):
+        target = step * (reach(v, step) - k + 1)
+        if k > 1:
+            slot = slot_of(v, step, k - 1)
+            arrived(ring1.at[s, v, slot], ring1_recv.at[s, v, slot])
+            add_into(s, v, target, [slot])
+        slot = slot_of(v, step, k)
+        source = own.at[own_piece(s, v, target, pl.ds(0, side))]
+        send(source, ring1.at[s, v, slot], ring1_recv.at[s, v, slot], neighbour(1 - s, step))
+
+    def same_plane(a, b):
+        return (a - b) % side == 0
+
+    done = []
+    for number, offset in enumerate(planes):
+        plane(offset)
+        if number > 0:
+            done.append(planes[number - 1])
+            join(planes[number - 1])
+            for v in (0, 1):
+                for step in (1, -1):
+                    if reach(v, step) >= 1 and same_plane(step * reach(v, step), planes[number - 1]):
+                        ring1_step(0, v, step, 1)
+    join(planes[-1])
+    for v in (0, 1):
+        for step in (1, -1):
+            if reach(v, step) >= 1:
+                ring1_step(1, v, step, 1)
+    for k in range(2, longest + 1):
+        for s in (0, 1):
+            for v in (0, 1):
+                for step in (1, -1):
+                    if k <= reach(v, step):
+                        ring1_step(s, v, step, k)
+
+    def last_piece(s, v, target):
+        spot = pl.ds(v * half_rows, half_rows), pl.ds(s * part, part)
+        if s == 0:
+            return (zpos, ring_order(lax.rem(ppos + target + 2 * side, side))) + spot
+        return (lax.rem(zpos + target + 2 * side, side), ring_order(ppos)) + spot
+
+    def ring2_step(s, v, step, k):
+        target = step * (reach(v, step) - k + 1)
+        index = last_piece(s, v, target)
+        if k > 1:
+            slot = slot_of(v, step, k - 1)
+            arrived(ring2.at[s, v, slot], ring2_recv.at[s, v, slot])
+            total = own[index].astype(jnp.float32) + ring2[s, v, slot].astype(jnp.float32)
+            own[index] = total.astype(jnp.bfloat16)
+        slot = slot_of(v, step, k)
+        send(own.at[index], ring2.at[s, v, slot], ring2_recv.at[s, v, slot], neighbour(s, step))
+
+    for s in (0, 1):
+        for v in (0, 1):
+            slots = []
+            for step in (1, -1):
+                if reach(v, step) >= 1:
+                    slot = slot_of(v, step, reach(v, step))
+                    arrived(ring1.at[s, v, slot], ring1_recv.at[s, v, slot])
+                    slots.append(slot)
+            add_into(s, v, 0, slots)
+            for step in (1, -1):
+                if reach(v, step) >= 1:
+                    ring2_step(s, v, step, 1)
+    for k in range(2, longest + 1):
+        for s in (0, 1):
+            for v in (0, 1):
+                for step in (1, -1):
+                    if k <= reach(v, step):
+                        ring2_step(s, v, step, k)
+    arrived(shared_peer, plane_recv.at[side])
+    for s in (0, 1):
+        for v in (0, 1):
+            spot = pl.ds(v * half_rows, half_rows), pl.ds(s * part, part)
+            total = own[last_piece(s, v, 0)].astype(jnp.float32)
+            for step in (1, -1):
+                if reach(v, step) >= 1:
+                    slot = slot_of(v, step, reach(v, step))
+                    arrived(ring2.at[s, v, slot], ring2_recv.at[s, v, slot])
+                    total += ring2[s, v, slot].astype(jnp.float32)
+            total += shared_own[spot] + shared_peer[spot]
+            out[spot] = total.astype(jnp.bfloat16)
+    for copy in pending:
+        copy.wait_send()
+
+
+def per_device_fused(
+    side, tokens, expert_ids, gate_values, w_gate, w_up, w_down, shared_gate, shared_up, shared_down
+):
+    rows, width = tokens.shape
+    n = side * side
+    half, part = width // 2, width // 4
+    fe = w_gate.shape[2]
+    weights = route_scale * gate_values / jnp.sum(gate_values, axis=1, keepdims=True)
+    chosen = expert_ids.T[:, None, :] == jnp.arange(n, dtype=jnp.int32)[None, :, None]
+    tab = jnp.sum(jnp.where(chosen, weights.T[:, None, :], 0.0), axis=0)
+    sends = 5 * (n - 1) + 4 * (n - 1) + 8 * (side - 1) + side + 1
+    dma = pltpu.SemaphoreType.DMA
+    bf, f32 = jnp.bfloat16, jnp.float32
+    anywhere = pl.BlockSpec(memory_space=pl.ANY)
+    return pl.pallas_call(
+        functools.partial(fused_kernel, side),
+        out_shape=jax.ShapeDtypeStruct((rows, half), bf),
+        in_specs=[anywhere] * 8,
+        out_specs=pl.BlockSpec(memory_space=pltpu.VMEM),
+        scratch_shapes=[
+            pltpu.VMEM((n * rows, width), bf),
+            pltpu.VMEM((n, n, rows), f32),
+            pltpu.VMEM((side, side, rows, half), bf),
+            pltpu.VMEM((side, side, rows, half), bf),
+            pltpu.VMEM((side, side, rows, half), bf),
+            pltpu.VMEM((side * rows, fe), bf),
+            pltpu.VMEM((width, fe), bf),
+            pltpu.VMEM((width, fe), bf),
+            pltpu.VMEM((fe, width), bf),
+            pltpu.VMEM((rows, half), f32),
+            pltpu.VMEM((rows, half), f32),
+            pltpu.VMEM((rows, half), f32),
+            pltpu.VMEM((2, 2, side - 1, side, rows // 2, part), bf),
+            pltpu.VMEM((2, 2, side - 1, rows // 2, part), bf),
+            dma((5,)),
+            dma((3, 2, n)),
+            dma((2, 2, n)),
+            dma((side + 1,)),
+            dma((2, 2, side - 1)),
+            dma((2, 2, side - 1)),
+            dma((sends,)),
+        ],
+        compiler_params=pltpu.CompilerParams(
+            collective_id=0, has_side_effects=True, vmem_limit_bytes=VMEM_BYTES
+        ),
+    )(tokens, tab, w_gate[0], w_up[0], w_down[0], shared_gate, shared_up, shared_down)
+
+
+def per_device(tokens, expert_ids, gate_values, w_gate, *rest):
+    n, cores = lax.axis_size("ep"), lax.axis_size("tp")
+    rows, width = tokens.shape
+    side = math.isqrt(n)
+    fe = w_gate.shape[2]
+    needed = 2 * n * rows * width * 5 // 2 + 6 * fe * width + n * rows * width
+    fits = side * side == n and side % 4 == 0 and cores == 2 and rows == LANES
+    fits = fits and w_gate.shape[0] == 1 and rest[2].shape[1] == fe
+    fits = fits and width % (4 * LANES) == 0 and width // 2 % 256 == 0 and fe % 256 == 0
+    if fits and needed < VMEM_BYTES:
+        return per_device_fused(side, tokens, expert_ids, gate_values, w_gate, *rest)
+    return per_device_routed(tokens, expert_ids, gate_values, w_gate, *rest)
+
+
 def solution(mesh):
     return jax.shard_map(
         per_device,

time: 534 us -> 188 us (0.35)
  waiting for transfers between devices: 278 us -> 0 us
  Pallas kernels: 0 us -> 183 us
  blocking collectives: 131 us -> 0 us
  other arithmetic: 36.9 us -> 2.69 us
  matrix products: 33.2 us -> 0 us
  local copies, waits for them, and re-layouts: 33.8 us -> 1.82 us
  between operations: 13.6 us -> 0.01 us
  starting transfers between devices: 7.23 us -> 0 us
    all_to_all x1 -> x0, waiting for transfers between devices: 205 us -> none  [per_device(): lax.all_to_all(partial_value.reshape(ep_count, capacity, model_width).ast...]
    pallas_call x0 -> x1, Pallas kernels: none -> 183 us  [per_device_fused(): pl.pallas_call(functools.partial(fused_kernel, side), out_shape=jax.Shape...]
    all_to_all x1 -> x0, blocking collectives: 131 us -> none  [per_device(): lax.all_to_all(outgoing, 'ep', split_axis=0, concat_axis=0, tiled=True)]
    reduce_scatter x1 -> x0, waiting for transfers between devices: 52.3 us -> none  [per_device(): lax.psum_scatter(routed + shared, 'tp', scatter_dimension=1, tiled=True)]
    dot_general x5 -> x0, matrix products: 33.2 us -> none  [the longest x2 14.2 us: expert_apply(): return jnp.dot(hidden, down_matrix, preferred_element_type=jnp.float32)]
    gather x2 -> x0, local copies, waits for them, and re-layouts: 27.4 us -> none  [the longest x1 20.7 us: combine_rows(): picked = jnp.take(returned.reshape(-1, feature_count), target, axis=0)]
    all_gather x1 -> x0, waiting for transfers between devices: 21.1 us -> none  [per_device(): arrived = lax.all_gather(parted, 'tp', axis=2, tiled=True)]
    reshape x1 -> x0, other arithmetic: 12.5 us -> none  [combine_rows(): picked = jnp.take(returned.reshape(-1, feature_count), target, axis=0)]
  transfers between devices with their start and end apart: 3 -> 0, of which waited for: 3 -> 0; matrix products, arithmetic and copies ran while one was open for 1% -> 0% of each run, Pallas kernels for 0% -> 0%
where the time goes in v1:
time: 188 us
  Pallas kernels  183 us (97%)
  other arithmetic  2.69 us (1%)
    pallas_call x1, Pallas kernels, per_device_fused(): pl.pallas_call(functools.partial(fused_kernel, side), out_shape=jax.Shape...  183 us

profile of v1, /device:TPU:0, one launch (start us, length us, event | category | flops | bytes accessed | tf_op | source)
XLA Modules:
  0.0 187.6 jit_solution(11650153036534275124)
XLA Ops:
  0.0 0.7 reduce_sum.18
  0.7 0.7 divide_bitcast_fusion
  1.4 1.3 select_reduce_fusion.tab
  2.7 183.1 %shard_map.91 = bf16[128,1792]{1,0:T(8,128)(2,1)} custom-call(bf16[128,3584]{1,0:T(8,128)(2,1)} %tok.1, f32[16,128]{1,0:T(8,128)} %select_reduce_fusion.tab, bf16[3584,512]{1,0:T(8,128)(2,1)} %bitcast.6, bf16[3584,512]{1,0:T(8,128)(2,1)} %bitcast.7, bf16[512,3584]{1,0:T(8,128)(2,1)} %bitcast.8, bf16[3584,512]{1,0:T(8,128)(2,1)} %s_gate.1, ...), custom_call_target="tpu_custom_call" | custom-call | tf_op jit(solution)/shard_map/pallas_call | solution.py:415
  185.8 1.8 copy.11
